TPU v7x, 32 devices: a whole 2x2x4 slice. The times are simulated.
32 devices in a mesh: dp: 8 (over z, x), feat: 4 (over y, core).
Axes of the slice: x: 2, y: 2, z: 4, core: 2. Of those that a mesh axis runs over, the one named last changes fastest.
Arguments:
- activations: bfloat16 [2048, 8192], P('dp', 'feat'), may hold values from -6 to 6
- cotangent: bfloat16 [2048, 1024], P('dp'), may hold values from -0.13183594 to 0.13183594
- weight: float32 [8192, 1024], P('feat'), may hold values from -0.0625 to 0.0625
- stats_old: float32 [4, 8, 4, 256, 256], P('feat', 'dp'), as said below
- owners: int32 [32, 4], replicated, may hold values from 0 to 7, as said below
- next_acts: bfloat16 [2048, 8192], P('dp', 'feat'), may hold values from -6 to 6
Outputs:
- weight_new: float32 [8192, 1024], P('feat')
- stats_new: float32 [4, 8, 4, 256, 256], P('feat', 'dp')
- next_out: bfloat16 [2048, 1024], P('dp', 'feat')
Inputs may be any that keep to these rules, and one draw needn't show every extreme that they name: `owners`: blocks are grouped by the index of feat that holds their rows (8192 / (256 * 4) row blocks a group); in every group each dp index owns at most 4 blocks, and some dp index owns exactly 4. `stats_old`: every slot holds a symmetric positive definite matrix; slots that no block maps to are not read.
All inputs are finite; a program needn't handle non-finite values.
Results may differ from a plain program's by a relative error of at most 0.02.
Values may be sent and summed in bfloat16 or wider, within the bound.
A program may use at most 128 MiB of HBM per device.

v0:
```python
import jax
import jax.numpy as jnp
from jax import lax
from jax.sharding import PartitionSpec as P

ITERS = 6
decay_rate = 0.9
step_rate = 0.01


def from_root(x, axis, root):
    mine = lax.axis_index(axis) == root
    return lax.psum(jnp.where(mine, x, jnp.zeros_like(x)), axis)


def newton_root(stats):
    width = stats.shape[0]
    identity = jnp.eye(width, dtype=jnp.float32)
    norm_value = jnp.sqrt(jnp.sum(stats * stats) + 1e-06)
    matrix = stats / norm_value
    iterate = identity
    for counter in range(ITERS):
        factor = (5.0 * identity - matrix) / 4.0
        factor_low = factor.astype(jnp.bfloat16)
        iterate = jnp.dot(
            iterate.astype(jnp.bfloat16), factor_low, preferred_element_type=jnp.float32
        )
        if counter + 1 < ITERS:
            square = jnp.dot(factor_low, factor_low, preferred_element_type=jnp.float32).astype(
                jnp.bfloat16
            )
            fourth = jnp.dot(square, square, preferred_element_type=jnp.float32).astype(
                jnp.bfloat16
            )
            matrix = jnp.dot(
                fourth, matrix.astype(jnp.bfloat16), preferred_element_type=jnp.float32
            )
    return iterate * norm_value ** (-0.25)


def update_stats(grad_block, old_stats):
    gram = (
        jnp.dot(grad_block, grad_block.T, preferred_element_type=jnp.float32) / grad_block.shape[0]
    )
    return decay_rate * old_stats + (1.0 - decay_rate) * gram


def block_at(matrix, block_id, col_blocks, width):
    row_start = block_id // col_blocks * width
    col_start = block_id % col_blocks * width
    return lax.dynamic_slice(matrix, (row_start, col_start), (width, width))


def body(activations, cotangent, weight, stats_old, owners, next_acts):
    width = stats_old.shape[-1]
    slots = stats_old.shape[2]
    rows_dev, columns = weight.shape
    row_blocks = rows_dev // width
    col_blocks = columns // width
    block_count = row_blocks * col_blocks
    partial_grad = jnp.einsum(
        "td,tc->dc", activations, cotangent, preferred_element_type=jnp.float32
    )
    summed = lax.psum(partial_grad, "dp")
    grad_low = summed.astype(jnp.bfloat16)
    feat_index = lax.axis_index("feat")
    data_index = lax.axis_index("dp")
    own_list = lax.dynamic_slice_in_dim(owners, feat_index * row_blocks, row_blocks, 0).reshape(
        block_count
    )
    is_mine = (own_list == data_index).astype(jnp.int32)
    slot_of = jnp.cumsum(is_mine) - is_mine
    block_ids = jnp.arange(block_count, dtype=jnp.int32)
    slot_pick = jnp.clip(slot_of, 0, slots - 1)
    stats_list = []
    renewed_list = []
    chosen_list = []
    for position in range(slots):
        picked = (is_mine == 1) & (slot_of == position)
        alive = jnp.any(picked)
        chosen = jnp.sum(jnp.where(picked, block_ids, 0))
        grad_block = block_at(grad_low, chosen, col_blocks, width)
        renewed = update_stats(grad_block, stats_old[0, 0, position])
        stats_list.append(jnp.where(alive, renewed, 0.0))
        renewed_list.append(renewed)
        chosen_list.append(chosen)
    root_list = [newton_root(renewed) for renewed in renewed_list]
    new_list = []
    fresh_list = []
    for root_matrix, chosen in zip(root_list, chosen_list):
        grad_block = block_at(grad_low, chosen, col_blocks, width)
        weight_block = block_at(weight, chosen, col_blocks, width)
        update = jnp.dot(
            root_matrix.astype(jnp.bfloat16), grad_block, preferred_element_type=jnp.float32
        )
        fresh_list.append(weight_block - step_rate * update)
    candidates = jnp.stack(fresh_list)
    for position in range(block_count):
        sending = lax.dynamic_index_in_dim(candidates, slot_pick[position], 0, keepdims=False)
        new_list.append(
            from_root(sending.astype(jnp.bfloat16), "dp", own_list[position]).astype(sending.dtype)
        )
    new_blocks = jnp.stack(new_list)
    weight_new = (
        new_blocks.reshape(row_blocks, col_blocks, width, width)
        .transpose(0, 2, 1, 3)
        .reshape(rows_dev, columns)
    )
    stats_out = jnp.stack(stats_list)[None, None]
    partial_next = jnp.dot(
        next_acts, weight_new.astype(jnp.bfloat16), preferred_element_type=jnp.float32
    )
    next_out = lax.psum_scatter(
        partial_next.astype(jnp.bfloat16), "feat", scatter_dimension=1, tiled=True
    )
    return (weight_new, stats_out, next_out)


def solution(mesh):
    placed = (
        P("dp", "feat"),
        P("dp", None),
        P("feat", None),
        P("feat", "dp", None, None, None),
        P(),
        P("dp", "feat"),
    )
    return jax.shard_map(
        body,
        mesh=mesh,
        in_specs=placed,
        out_specs=(P("feat", None), P("feat", "dp", None, None, None), P("dp", "feat")),
        check_vma=False,
    )
```

profile of v0, /device:TPU:0, one launch (start us, length us, event | category | flops | bytes accessed | tf_op | source)
XLA Modules:
  0.0 700.2 jit_solution(15082206161460627291)
XLA Ops:
  13.1 5.7 fusion.363
  18.9 328.1 %all-reduce.5 = bf16[2048,1024]{1,0:T(8,128)(2,1)} all-reduce(f32[2048,1024]{1,0:T(8,128)} %fusion.363), channel_id=1, replica_groups=mesh['dp'=8,'feat'=4] {'dp'}, use_global_device_ids=true, to_apply=%region_2.3 | all-reduce | flops 2097152 | bytes 12582912 | tf_op jit(solution)/shard_map/psum | solution.py:64
  347.0 1.8 multiply_reduce_fusion
  354.6 1.9 multiply_reduce_fusion.1
  363.3 1.9 multiply_reduce_fusion.2
  370.9 1.8 multiply_reduce_fusion.3
  421.7 1.2 convolution_convert_fusion.6
  425.8 1.2 fusion.2
  427.4 1.2 fusion.6
  431.4 1.2 fusion.10
  435.5 1.2 fusion.14
  477.7 1.0 fusion.78
  478.8 1.1 fusion.87
  479.8 1.1 fusion.96
  481.2 166.1 %all-reduce.4.cloned.1.call-done = (bf16[1,256,256]{2,1,0:T(8,128)(2,1)}, bf16[1,256,256]{2,1,0:T(8,128)(2,1)}, bf16[1,256,256]{2,1,0:T(8,128)(2,1)}, bf16[1,256...) async-done(((bf16[1,256,256]{2,1,0:T(8,128)(2,1)}, ...) | async-done | bytes 4194320 | tf_op jit(solution)/shard_map/psum | solution.py:13
  647.4 1.1 constant_dynamic-update-slice_fusion.31
  662.7 3.2 copy.15
  666.0 1.0 copy.18
  667.1 1.9 copy-done.2
  669.0 2.1 fusion
  671.2 1.0 maximum_bitcast_fusion
  672.2 6.6 reshape.195
  678.8 12.9 %reduce-scatter.2.cloned.1.call-done = bf16[256,256]{0,1:T(8,128)(2,1)} async-done(((bf16[256,1024]{0,1:T(8,128)(2,1)}), bf16[256,256]{0,1:T(8,128)(2,1)}) %reduce-scatter.2.cloned.1.call-update) | async-done | bytes 131088 | tf_op jit(solution)/shard_map/reduce_scatter | solution.py:113
  691.7 1.7 copy.16
  (156 shorter events, 43.8 us)
Async XLA Ops:
  7.2 6.0 copy-start
  7.2 640.1 %all-reduce.4.cloned.1.call-start = ((), (), s32[]{:S(2)}) async-start(), calls=%async_computation.2 | async-start | bytes 8388608 | tf_op jit(solution)/shard_map/psum | solution.py:13
  18.9 328.1 %copy-start.3 = (f32[1,1,4,256,256]{4,3,2,1,0:T(8,128)S(1)}, f32[1,1,4,256,256]{4,3,2,1,0:T(8,128)}, u32[]{:S(2)}) copy-start(f32[1,1,4,256,256]{4,3,2,1,0:T(8,128)} %param.9) | copy-start | bytes 3145732
  419.8 5.3 copy-start.21
  425.4 5.3 copy-start.22
  429.4 5.3 copy-start.23
  480.9 210.8 %reduce-scatter.2.cloned.1.call-start = ((), (), s32[]{:S(2)}) async-start(), calls=%async_computation.1 | async-start | bytes 655360 | tf_op jit(solution)/shard_map/reduce_scatter | solution.py:113
  647.3 15.0 %copy-start.19 = (bf16[1,256,256]{2,1,0:T(8,128)(2,1)S(1)}, bf16[1,256,256]{2,1,0:T(8,128)(2,1)}, u32[]{:S(2)}) copy-start(bf16[1,256,256]{2,1,0:T(8,128)(2,1)} %get-tuple-element.25) | copy-start | bytes 393220
  647.3 15.0 %copy-start.18 = (bf16[1,256,256]{2,1,0:T(8,128)(2,1)S(1)}, bf16[1,256,256]{2,1,0:T(8,128)(2,1)}, u32[]{:S(2)}) copy-start(bf16[1,256,256]{2,1,0:T(8,128)(2,1)} %get-tuple-element.26) | copy-start | bytes 393220
  647.3 15.0 %copy-start.17 = (bf16[1,256,256]{2,1,0:T(8,128)(2,1)S(1)}, bf16[1,256,256]{2,1,0:T(8,128)(2,1)}, u32[]{:S(2)}) copy-start(bf16[1,256,256]{2,1,0:T(8,128)(2,1)} %get-tuple-element.27) | copy-start | bytes 393220
  647.3 15.0 %copy-start.16 = (bf16[1,256,256]{2,1,0:T(8,128)(2,1)S(1)}, bf16[1,256,256]{2,1,0:T(8,128)(2,1)}, u32[]{:S(2)}) copy-start(bf16[1,256,256]{2,1,0:T(8,128)(2,1)} %get-tuple-element.28) | copy-start | bytes 393220
  647.3 15.1 %copy-start.15 = (bf16[1,256,256]{2,1,0:T(8,128)(2,1)S(1)}, bf16[1,256,256]{2,1,0:T(8,128)(2,1)}, u32[]{:S(2)}) copy-start(bf16[1,256,256]{2,1,0:T(8,128)(2,1)} %get-tuple-element.29) | copy-start | bytes 393220
  647.3 15.1 %copy-start.14 = (bf16[1,256,256]{2,1,0:T(8,128)(2,1)S(1)}, bf16[1,256,256]{2,1,0:T(8,128)(2,1)}, u32[]{:S(2)}) copy-start(bf16[1,256,256]{2,1,0:T(8,128)(2,1)} %get-tuple-element.30) | copy-start | bytes 393220
  647.3 15.1 %copy-start.13 = (bf16[1,256,256]{2,1,0:T(8,128)(2,1)S(1)}, bf16[1,256,256]{2,1,0:T(8,128)(2,1)}, u32[]{:S(2)}) copy-start(bf16[1,256,256]{2,1,0:T(8,128)(2,1)} %get-tuple-element.31) | copy-start | bytes 393220
  647.3 15.1 %copy-start.12 = (bf16[1,256,256]{2,1,0:T(8,128)(2,1)S(1)}, bf16[1,256,256]{2,1,0:T(8,128)(2,1)}, u32[]{:S(2)}) copy-start(bf16[1,256,256]{2,1,0:T(8,128)(2,1)} %get-tuple-element.32) | copy-start | bytes 393220
  647.4 15.2 %copy-start.11 = (bf16[1,256,256]{2,1,0:T(8,128)(2,1)S(1)}, bf16[1,256,256]{2,1,0:T(8,128)(2,1)}, u32[]{:S(2)}) copy-start(bf16[1,256,256]{2,1,0:T(8,128)(2,1)} %get-tuple-element.33) | copy-start | bytes 393220
  647.4 15.2 %copy-start.10 = (bf16[1,256,256]{2,1,0:T(8,128)(2,1)S(1)}, bf16[1,256,256]{2,1,0:T(8,128)(2,1)}, u32[]{:S(2)}) copy-start(bf16[1,256,256]{2,1,0:T(8,128)(2,1)} %get-tuple-element.34) | copy-start | bytes 393220
  647.4 15.2 %copy-start.9 = (bf16[1,256,256]{2,1,0:T(8,128)(2,1)S(1)}, bf16[1,256,256]{2,1,0:T(8,128)(2,1)}, u32[]{:S(2)}) copy-start(bf16[1,256,256]{2,1,0:T(8,128)(2,1)} %get-tuple-element.35) | copy-start | bytes 393220
  647.4 15.2 %copy-start.8 = (bf16[1,256,256]{2,1,0:T(8,128)(2,1)S(1)}, bf16[1,256,256]{2,1,0:T(8,128)(2,1)}, u32[]{:S(2)}) copy-start(bf16[1,256,256]{2,1,0:T(8,128)(2,1)} %get-tuple-element.36) | copy-start | bytes 393220
  647.4 15.2 %copy-start.7 = (bf16[1,256,256]{2,1,0:T(8,128)(2,1)S(1)}, bf16[1,256,256]{2,1,0:T(8,128)(2,1)}, u32[]{:S(2)}) copy-start(bf16[1,256,256]{2,1,0:T(8,128)(2,1)} %get-tuple-element.37) | copy-start | bytes 393220
  647.4 15.2 %copy-start.6 = (bf16[1,256,256]{2,1,0:T(8,128)(2,1)S(1)}, bf16[1,256,256]{2,1,0:T(8,128)(2,1)}, u32[]{:S(2)}) copy-start(bf16[1,256,256]{2,1,0:T(8,128)(2,1)} %get-tuple-element.38) | copy-start | bytes 393220
  647.4 15.3 %copy-start.5 = (bf16[1,256,256]{2,1,0:T(8,128)(2,1)S(1)}, bf16[1,256,256]{2,1,0:T(8,128)(2,1)}, u32[]{:S(2)}) copy-start(bf16[1,256,256]{2,1,0:T(8,128)(2,1)} %get-tuple-element.39) | copy-start | bytes 393220
  647.4 15.3 %copy-start.4 = (bf16[1,256,256]{2,1,0:T(8,128)(2,1)S(1)}, bf16[1,256,256]{2,1,0:T(8,128)(2,1)}, u32[]{:S(2)}) copy-start(bf16[1,256,256]{2,1,0:T(8,128)(2,1)} %get-tuple-element.40) | copy-start | bytes 393220
  671.1 22.2 %copy-start.1 = (bf16[256,2048]{1,0:T(8,128)(2,1)S(1)}, bf16[256,2048]{1,0:T(8,128)(2,1)}, u32[]{:S(2)}) copy-start(bf16[256,2048]{1,0:T(8,128)(2,1)} %param.6) | copy-start | bytes 3145732
  (2 other events, 4.9 us)
Sparse Core Ops, SparseCore 0:
  481.0 166.2 all-reduce.3
  671.3 20.4 reduce-scatter.1
where the time goes:
time: 702 us; the launch traced here: 700 us
  blocking collectives  328 us (47%)
  waiting for transfers between devices  179 us (25%)
  between operations  108 us (15%)
  matrix products  40.3 us (6%)
  local copies, waits for them, and re-layouts  27 us (4%)
  other arithmetic  17.4 us (2%)
    psum x1, blocking collectives, body(): summed = lax.psum(partial_grad, 'dp')  328 us
    psum x1, waiting for transfers between devices, from_root(): return lax.psum(jnp.where(mine, x, jnp.zeros_like(x)), axis)  166 us
    unnamed x82, local copies, waits for them, and re-layouts  19.8 us
  transfers between devices with their start and end apart: 2, of which 2 were waited for; matrix products, arithmetic and copies ran while one was open for 1% of the time, Pallas kernels for 0%

commit v1 on v0

--- a/solution.py
+++ b/solution.py
@@ -2,6 +2,7 @@
 import jax.numpy as jnp
 from jax import lax
 from jax.sharding import PartitionSpec as P
+from jax.lax import axis_size, ppermute
 
 ITERS = 6
 decay_rate = 0.9
@@ -61,7 +62,12 @@
     partial_grad = jnp.einsum(
         "td,tc->dc", activations, cotangent, preferred_element_type=jnp.float32
     )
-    summed = lax.psum(partial_grad, "dp")
+    summed, x_next = (partial_grad, 0)
+    parts_n = axis_size("dp")
+    while 1 << x_next < parts_n:
+        right_arr = ppermute(summed, "dp", [(ii, ii ^ 1 << x_next) for ii in range(parts_n)])
+        summed = summed + right_arr
+        x_next = x_next + 1
     grad_low = summed.astype(jnp.bfloat16)
     feat_index = lax.axis_index("feat")
     data_index = lax.axis_index("dp")

time: 702 us -> 1050 us (1.50)
  waiting for transfers between devices: 179 us -> 805 us
  blocking collectives: 328 us -> 0 us
  other arithmetic: 17.4 us -> 49.1 us
    ppermute x0 -> x3, waiting for transfers between devices: none -> 624 us  [body(): ppermute(summed, 'dp', [(ii, ii ^ 1 << x_next) for ii in range(parts_n)])]
    psum x1 -> x0, blocking collectives: 328 us -> none  [body(): summed = lax.psum(partial_grad, 'dp')]
    add x0 -> x2, other arithmetic: none -> 24.3 us  [body(): summed = summed + right_arr]
    unnamed x82 -> x86, local copies, waits for them, and re-layouts: 19.8 us -> 26.4 us
  transfers between devices with their start and end apart: 2 -> 5, of which waited for: 2 -> 5; matrix products, arithmetic and copies ran while one was open for 1% -> 1% of each run, Pallas kernels for 0% -> 0%
where the time goes in v1:
time: 1050 us; the launch traced here: 1040 us
  waiting for transfers between devices  805 us (77%)
  between operations  108 us (10%)
  other arithmetic  49.1 us (5%)
  matrix products  41.9 us (4%)
  local copies, waits for them, and re-layouts  32.8 us (3%)
    ppermute x3, waiting for transfers between devices, body(): ppermute(summed, 'dp', [(ii, ii ^ 1 << x_next) for ii in range(parts_n)])  624 us
    psum x1, waiting for transfers between devices, from_root(): return lax.psum(jnp.where(mine, x, jnp.zeros_like(x)), axis)  169 us
    unnamed x86, local copies, waits for them, and re-layouts  26.4 us
    add x2, other arithmetic, body(): summed = summed + right_arr  24.3 us
  transfers between devices with their start and end apart: 5, of which 5 were waited for; matrix products, arithmetic and copies ran while one was open for 1% of the time, Pallas kernels for 0%

profile of v1, /device:TPU:0, one launch (start us, length us, event | category | flops | bytes accessed | tf_op | source)
XLA Modules:
  0.0 1044.4 jit_solution(18159380219347900814)
XLA Ops:
  8.4 2.3 fusion.363
  10.7 3.4 copy-done.2
  14.1 3.0 collective-permute-start
  17.1 180.6 %collective-permute-done = f32[2048,1024]{1,0:T(8,128)} collective-permute-done((f32[2048,1024]{1,0:T(8,128)S(1)}, f32[2048,1024]{1,0:T(8,128)}, u32[]{:S(2)}, u32[]{:S(2)}) %collective-permute-start) | collective-permute-done | bytes 8388640 | tf_op jit(solution)/shard_map/ppermute | solution.py:68
  197.7 12.1 %add.272 = f32[2048,1024]{1,0:T(8,128)} add(f32[2048,1024]{1,0:T(8,128)} %copy-done.2, f32[2048,1024]{1,0:T(8,128)} %collective-permute-done) | non-fusion elementwise | flops 2097152 | bytes 25165824 | tf_op jit(solution)/shard_map/add | solution.py:69
  209.8 1.8 collective-permute-start.1
  211.6 180.1 %collective-permute-done.1 = f32[2048,1024]{1,0:T(8,128)} collective-permute-done((f32[2048,1024]{1,0:T(8,128)}, f32[2048,1024]{1,0:T(8,128)}, u32[]{:S(2)}, u32[]{:S(2)}) %collective-permute-start.1) | collective-permute-done | bytes 8388640 | tf_op jit(solution)/shard_map/ppermute | solution.py:68
  391.7 12.1 %add.273 = f32[2048,1024]{1,0:T(8,128)} add(f32[2048,1024]{1,0:T(8,128)} %add.272, f32[2048,1024]{1,0:T(8,128)} %collective-permute-done.1) | non-fusion elementwise | flops 2097152 | bytes 25165824 | tf_op jit(solution)/shard_map/add | solution.py:69
  403.9 2.6 collective-permute-start.2
  502.7 263.0 %collective-permute-done.2 = f32[2048,1024]{1,0:T(8,128)} collective-permute-done((f32[2048,1024]{1,0:T(8,128)}, f32[2048,1024]{1,0:T(8,128)}, u32[]{:S(2)}, u32[]{:S(2)}) %collective-permute-start.2) | collective-permute-done | bytes 8388640 | tf_op jit(solution)/shard_map/ppermute | solution.py:68
  765.6 7.3 add_convert_fusion
  772.9 2.0 copy-done.4
  779.9 1.9 multiply_reduce_fusion.1
  786.0 1.9 multiply_reduce_fusion.2
  791.5 1.9 multiply_reduce_fusion.3
  803.6 1.9 convolution_convert_fusion.21
  807.1 1.2 fusion.22
  822.9 168.5 %all-reduce.3.cloned.1.call-done = (bf16[1,256,256]{2,1,0:T(8,128)(2,1)}, bf16[1,256,256]{2,1,0:T(8,128)(2,1)}, bf16[1,256,256]{2,1,0:T(8,128)(2,1)}, bf16[1,256...) async-done(((bf16[1,256,256]{2,1,0:T(8,128)(2,1)}, ...) | async-done | bytes 4194320 | tf_op jit(solution)/shard_map/psum | solution.py:14
  1006.9 3.2 copy.15
  1011.2 1.9 copy-done.3
  1013.2 2.1 fusion
  1016.4 6.6 reshape.195
  1023.0 12.9 %reduce-scatter.2.cloned.1.call-done = bf16[256,256]{0,1:T(8,128)(2,1)} async-done(((bf16[256,1024]{0,1:T(8,128)(2,1)}), bf16[256,256]{0,1:T(8,128)(2,1)}) %reduce-scatter.2.cloned.1.call-update) | async-done | bytes 131088 | tf_op jit(solution)/shard_map/reduce_scatter | solution.py:119
  1035.9 1.7 copy.16
  (168 shorter events, 60.3 us)
Async XLA Ops:
  7.2 984.3 %all-reduce.3.cloned.1.call-start = ((), (), s32[]{:S(2)}) async-start(), calls=%async_computation.2 | async-start | bytes 8388608 | tf_op jit(solution)/shard_map/psum | solution.py:14
  14.1 183.5 %collective-permute-start = (f32[2048,1024]{1,0:T(8,128)S(1)}, f32[2048,1024]{1,0:T(8,128)}, u32[]{:S(2)}, u32[]{:S(2)}) collective-permute-start(f32[2048,1024]{1,0:T(8,128)S(1)} %fusion.363), channel_id=1, source_target_pairs={{0,4},{4,0},{8,12},{12,8},{16,20},{20,16},{24,28},{28,24},{1,5},{5... | collective-permute-start | bytes 25165832 | tf_op jit(solution)/shard_map/ppermute | solution.py:68
  209.8 196.6 %copy-start.23 = (s32[32,4]{0,1:T(4,128)S(1)}, s32[32,4]{0,1:T(4,128)}, u32[]{:S(2)}) copy-start(s32[32,4]{0,1:T(4,128)} %param.10) | copy-start | bytes 1540
  209.8 181.9 %collective-permute-start.1 = (f32[2048,1024]{1,0:T(8,128)}, f32[2048,1024]{1,0:T(8,128)}, u32[]{:S(2)}, u32[]{:S(2)}) collective-permute-start(f32[2048,1024]{1,0:T(8,128)} %add.272), channel_id=1, source_target_pairs={{0,8},{4,12},{8,0},{12,4},{16,24},{20,28},{24,16},{28,20},{1,9},{5... | collective-permute-start | bytes 25165832 | tf_op jit(solution)/shard_map/ppermute | solution.py:68
  403.9 361.7 %collective-permute-start.2 = (f32[2048,1024]{1,0:T(8,128)}, f32[2048,1024]{1,0:T(8,128)}, u32[]{:S(2)}, u32[]{:S(2)}) collective-permute-start(f32[2048,1024]{1,0:T(8,128)} %add.273), channel_id=1, source_target_pairs={{0,16},{4,20},{8,24},{12,28},{16,0},{20,4},{24,8},{28,12},{1,17},{... | collective-permute-start | bytes 25165832 | tf_op jit(solution)/shard_map/ppermute | solution.py:68
  502.7 272.3 %copy-start.5 = (f32[1,1,4,256,256]{4,3,2,1,0:T(8,128)S(1)}, f32[1,1,4,256,256]{4,3,2,1,0:T(8,128)}, u32[]{:S(2)}) copy-start(f32[1,1,4,256,256]{4,3,2,1,0:T(8,128)} %param.9) | copy-start | bytes 3145732
  822.7 213.2 %reduce-scatter.2.cloned.1.call-start = ((), (), s32[]{:S(2)}) async-start(), calls=%async_computation.1 | async-start | bytes 655360 | tf_op jit(solution)/shard_map/reduce_scatter | solution.py:119
  991.5 15.0 %copy-start.22 = (bf16[1,256,256]{2,1,0:T(8,128)(2,1)S(1)}, bf16[1,256,256]{2,1,0:T(8,128)(2,1)}, u32[]{:S(2)}) copy-start(bf16[1,256,256]{2,1,0:T(8,128)(2,1)} %get-tuple-element.25) | copy-start | bytes 393220
  991.5 15.0 %copy-start.21 = (bf16[1,256,256]{2,1,0:T(8,128)(2,1)S(1)}, bf16[1,256,256]{2,1,0:T(8,128)(2,1)}, u32[]{:S(2)}) copy-start(bf16[1,256,256]{2,1,0:T(8,128)(2,1)} %get-tuple-element.26) | copy-start | bytes 393220
  991.5 15.0 %copy-start.20 = (bf16[1,256,256]{2,1,0:T(8,128)(2,1)S(1)}, bf16[1,256,256]{2,1,0:T(8,128)(2,1)}, u32[]{:S(2)}) copy-start(bf16[1,256,256]{2,1,0:T(8,128)(2,1)} %get-tuple-element.27) | copy-start | bytes 393220
  991.5 15.0 %copy-start.19 = (bf16[1,256,256]{2,1,0:T(8,128)(2,1)S(1)}, bf16[1,256,256]{2,1,0:T(8,128)(2,1)}, u32[]{:S(2)}) copy-start(bf16[1,256,256]{2,1,0:T(8,128)(2,1)} %get-tuple-element.28) | copy-start | bytes 393220
  991.5 15.1 %copy-start.18 = (bf16[1,256,256]{2,1,0:T(8,128)(2,1)S(1)}, bf16[1,256,256]{2,1,0:T(8,128)(2,1)}, u32[]{:S(2)}) copy-start(bf16[1,256,256]{2,1,0:T(8,128)(2,1)} %get-tuple-element.29) | copy-start | bytes 393220
  991.5 15.1 %copy-start.17 = (bf16[1,256,256]{2,1,0:T(8,128)(2,1)S(1)}, bf16[1,256,256]{2,1,0:T(8,128)(2,1)}, u32[]{:S(2)}) copy-start(bf16[1,256,256]{2,1,0:T(8,128)(2,1)} %get-tuple-element.30) | copy-start | bytes 393220
  991.5 15.1 %copy-start.16 = (bf16[1,256,256]{2,1,0:T(8,128)(2,1)S(1)}, bf16[1,256,256]{2,1,0:T(8,128)(2,1)}, u32[]{:S(2)}) copy-start(bf16[1,256,256]{2,1,0:T(8,128)(2,1)} %get-tuple-element.31) | copy-start | bytes 393220
  991.5 15.1 %copy-start.15 = (bf16[1,256,256]{2,1,0:T(8,128)(2,1)S(1)}, bf16[1,256,256]{2,1,0:T(8,128)(2,1)}, u32[]{:S(2)}) copy-start(bf16[1,256,256]{2,1,0:T(8,128)(2,1)} %get-tuple-element.32) | copy-start | bytes 393220
  991.5 15.2 %copy-start.14 = (bf16[1,256,256]{2,1,0:T(8,128)(2,1)S(1)}, bf16[1,256,256]{2,1,0:T(8,128)(2,1)}, u32[]{:S(2)}) copy-start(bf16[1,256,256]{2,1,0:T(8,128)(2,1)} %get-tuple-element.33) | copy-start | bytes 393220
  991.5 15.2 %copy-start.13 = (bf16[1,256,256]{2,1,0:T(8,128)(2,1)S(1)}, bf16[1,256,256]{2,1,0:T(8,128)(2,1)}, u32[]{:S(2)}) copy-start(bf16[1,256,256]{2,1,0:T(8,128)(2,1)} %get-tuple-element.34) | copy-start | bytes 393220
  991.5 15.2 %copy-start.12 = (bf16[1,256,256]{2,1,0:T(8,128)(2,1)S(1)}, bf16[1,256,256]{2,1,0:T(8,128)(2,1)}, u32[]{:S(2)}) copy-start(bf16[1,256,256]{2,1,0:T(8,128)(2,1)} %get-tuple-element.35) | copy-start | bytes 393220
  991.5 15.2 %copy-start.11 = (bf16[1,256,256]{2,1,0:T(8,128)(2,1)S(1)}, bf16[1,256,256]{2,1,0:T(8,128)(2,1)}, u32[]{:S(2)}) copy-start(bf16[1,256,256]{2,1,0:T(8,128)(2,1)} %get-tuple-element.36) | copy-start | bytes 393220
  991.6 15.2 %copy-start.10 = (bf16[1,256,256]{2,1,0:T(8,128)(2,1)S(1)}, bf16[1,256,256]{2,1,0:T(8,128)(2,1)}, u32[]{:S(2)}) copy-start(bf16[1,256,256]{2,1,0:T(8,128)(2,1)} %get-tuple-element.37) | copy-start | bytes 393220
  991.6 15.2 %copy-start.9 = (bf16[1,256,256]{2,1,0:T(8,128)(2,1)S(1)}, bf16[1,256,256]{2,1,0:T(8,128)(2,1)}, u32[]{:S(2)}) copy-start(bf16[1,256,256]{2,1,0:T(8,128)(2,1)} %get-tuple-element.38) | copy-start | bytes 393220
  991.6 15.3 %copy-start.8 = (bf16[1,256,256]{2,1,0:T(8,128)(2,1)S(1)}, bf16[1,256,256]{2,1,0:T(8,128)(2,1)}, u32[]{:S(2)}) copy-start(bf16[1,256,256]{2,1,0:T(8,128)(2,1)} %get-tuple-element.39) | copy-start | bytes 393220
  991.6 15.3 %copy-start.7 = (bf16[1,256,256]{2,1,0:T(8,128)(2,1)S(1)}, bf16[1,256,256]{2,1,0:T(8,128)(2,1)}, u32[]{:S(2)}) copy-start(bf16[1,256,256]{2,1,0:T(8,128)(2,1)} %get-tuple-element.40) | copy-start | bytes 393220
  1015.3 22.2 %copy-start.1 = (bf16[256,2048]{1,0:T(8,128)(2,1)S(1)}, bf16[256,2048]{1,0:T(8,128)(2,1)}, u32[]{:S(2)}) copy-start(bf16[256,2048]{1,0:T(8,128)(2,1)} %param.6) | copy-start | bytes 3145732
  (7 other events, 25.9 us)
Sparse Core Ops, SparseCore 0:
  822.8 168.6 all-reduce.2
  1015.4 20.4 reduce-scatter.1
